TPU v7x, 32 devices: a whole 2x2x4 slice. The times are simulated.
32 devices in a mesh: ev: 8 (over z, y), pol: 4 (over x, core).
Axes of the slice: x: 2, y: 2, z: 4, core: 2. Of those that a mesh axis runs over, the one named last changes fastest.
Arguments:
- ground_up: bfloat16 [768, 128, 128], P('pol', 'ev'), may hold values from 1.9907951e-05 to 0.0019989014
- loc_deductible: bfloat16 [768, 128], P('pol'), may hold values from 0 to 0.00029945374
- loc_limit: bfloat16 [768, 128], P('pol'), may hold values from 0.00049972534 to 0.0014953613
- block_policy: int32 [768], P('pol'), may hold values from 0 to 255, as said below
- policy_deductible: float32 [256], P('pol'), may hold values from 0.02 to 0.12
- policy_limit: float32 [256], P('pol'), may hold values from 0.05 to 0.2
- policy_share: float32 [256], P('pol'), may hold values from 0.3 to 1
- policy_summary: int32 [256], P('pol'), may hold values from 0 to 31
- occurrence: int32 [128, 64], P('ev'), may hold values from 0 to 8191
Outputs:
- year_loss: float32 [32, 8192], P('pol', 'ev')
Inputs may be any that keep to these rules, and one draw needn't show every extreme that they name: `block_policy`: policy q is owned by index q // 64 of pol. Among the 192 blocks held by one index of pol, at most 72 belong to policies of any one owner; in every draw some owner gets exactly 72 blocks from every index of pol.
All inputs are finite; a program needn't handle non-finite values.
Results may differ from a plain program's by a relative error of at most 0.0003.
Values sent between devices are 32-bit elements; how exact they have to be, the bound alone decides.
A program may use at most 64 MiB of HBM per device.

v0:
```python
import jax
import jax.numpy as jnp
from jax import lax
from jax.sharding import PartitionSpec as P

SUMM = 32
YR_DEV = 1024


def block_totals(ground_up, loc_deductible, loc_limit):
    lower = loc_deductible.astype(jnp.float32)[:, None, :]
    upper = loc_limit.astype(jnp.float32)[:, None, :]
    net_loss = jnp.minimum(jnp.maximum(ground_up.astype(jnp.float32) - lower, 0.0), upper)
    return jnp.sum(net_loss, axis=2)


def per_device(
    ground_up,
    loc_deductible,
    loc_limit,
    block_policy,
    policy_deductible,
    policy_limit,
    policy_share,
    policy_summary,
    occurrence,
):
    owners = lax.axis_size("pol")
    per_owner = policy_share.shape[0]
    totals = block_totals(ground_up, loc_deductible, loc_limit)
    membership = (
        block_policy[:, None] == jnp.arange(per_owner * owners, dtype=jnp.int32)[None, :]
    ).astype(jnp.float32)
    partial_ground = jnp.dot(
        totals.T, membership, precision=lax.Precision.HIGHEST, preferred_element_type=jnp.float32
    )
    policy_ground = lax.psum_scatter(partial_ground, "pol", scatter_dimension=1, tiled=True)
    policy_losses = policy_share * jnp.minimum(
        jnp.maximum(policy_ground - policy_deductible, 0.0), policy_limit
    )
    summary_map = (policy_summary[:, None] == jnp.arange(SUMM, dtype=jnp.int32)[None, :]).astype(
        jnp.float32
    )
    summary_loss = jnp.dot(
        policy_losses,
        summary_map,
        precision=lax.Precision.HIGHEST,
        preferred_element_type=jnp.float32,
    )
    own_summary = lax.psum_scatter(summary_loss, "pol", scatter_dimension=1, tiled=True)
    every_summary = lax.all_gather(own_summary, "ev", axis=0, tiled=True)
    every_year = lax.all_gather(occurrence, "ev", axis=0, tiled=True)
    first_year = lax.axis_index("ev") * YR_DEV
    shifted = every_year - first_year
    inside = (shifted >= 0) & (shifted < YR_DEV)
    placed = jnp.where(inside, shifted, 0)
    weight = inside.reshape(-1).astype(jnp.float32)[:, None]
    repeated = jnp.repeat(every_summary, every_year.shape[1], axis=0) * weight
    empty = jnp.zeros((every_summary.shape[1], YR_DEV), jnp.float32)
    year_loss = empty.at[:, placed.reshape(-1)].add(repeated.T)
    return year_loss


def solution(mesh):
    placed = (
        P("pol", "ev", None),
        P("pol", None),
        P("pol", None),
        P("pol"),
        P("pol"),
        P("pol"),
        P("pol"),
        P("pol"),
        P("ev", None),
    )
    return jax.shard_map(
        per_device, mesh=mesh, in_specs=placed, out_specs=P("pol", "ev"), check_vma=False
    )
```

profile of v0, /device:TPU:0, one launch (start us, length us, event | category | flops | bytes accessed | tf_op | source)
XLA Modules:
  0.0 149.6 jit_solution(6546198905885632282)
XLA Ops:
  6.5 0.0 reduce-scatter.4.cloned.1.call-start
  6.5 0.8 convert_element_type.22
  7.3 0.8 convert_element_type.23
  8.2 1.6 %minimum_reduce_fusion = f32[192,16]{1,0:T(8,128)S(1)} fusion(bf16[192,16,128]{2,1,0:T(8,128)(2,1)} %param.9, f32[192,128]{1,0:T(8,128)S(1)} %convert_element_type.23, f32[192,128]{1,0:T(8,128)S(1)} %convert_element_type.22), kind=kLoop, calls=%fused_computation.2 | loop fusion | flops 1963008 | bytes 995328 | tf_op jit(solution)/shard_map/reduce_sum | solution.py:14
  9.8 1.8 %convolution_bitcast_fusion = f32[256,16]{1,0:T(8,128)} fusion(f32[192,16]{1,0:T(8,128)S(1)} %minimum_reduce_fusion, s32[192]{0:T(256)} %param.12), kind=kOutput, calls=%fused_computation.3 | convolution fusion | flops 9486336 | bytes 29440
  11.6 0.0 reduce-scatter.4.cloned.1.call-update
  11.6 32.6 %all_gather.6 = s32[128,64]{1,0:T(8,128)S(1)} all-gather(s32[16,64]{1,0:T(8,128)} %param.17), channel_id=1, replica_groups=mesh['ev'=8,'pol'=4] {'ev'}, dimensions={0}, use_global_device_ids=true | all-gather | bytes 36864 | tf_op jit(solution)/shard_map/all_gather | solution.py:52
  44.2 0.1 reshape.49
  44.4 0.1 reshape.51
  44.5 1.2 dynamic-slice
  46.4 0.0 reduce-scatter.4.cloned.1.call-done
  46.4 0.8 copy.19
  47.2 1.0 fusion.4
  48.2 10.1 %all-reduce = f32[16,32]{0,1:T(8,128)S(1)} all-reduce(f32[16,32]{0,1:T(8,128)S(1)} %fusion.4), channel_id=3, replica_groups=mesh['ev'=8,'pol'=4] {'pol'}, use_global_device_ids=true, to_apply=%region_2.0.clone | all-reduce | flops 512 | bytes 4096
  58.3 30.6 %all-gather = f32[8,16,8]{1,2,0:T(8,128)S(1)} all-gather(f32[1,16,8]{1,2,0:T(8,128)S(1)} %dynamic-slice_bitcast_fusion), channel_id=1, replica_groups=mesh['ev'=8,'pol'=4] {'ev'}, dimensions={0}, use_global_device_ids=true | all-gather | bytes 4608 | tf_op jit(solution)/shard_map/all_gather | solution.py:51
  88.9 0.1 copy.17
  89.0 2.6 %bitcast_multiply_fusion = f32[8192,8]{1,0:T(8,128)} fusion(f32[8192]{0:T(1024)S(1)} %reshape.51, f32[128,8]{1,0:T(8,128)S(1)} %bitcast.11), kind=kLoop, calls=%fused_computation.1 | loop fusion | flops 65536 | bytes 299008 | tf_op jit(solution)/shard_map/mul | solution.py:58
  91.5 50.4 %scatter_custom_fusion = f32[8,1024]{0,1:T(8,128)S(1)} fusion(s32[8192]{0:T(1024)S(1)} %bitcast.13, f32[8192,8]{1,0:T(8,128)} %bitcast_multiply_fusion, f32[]{:T(128)} %constant.5.clone.1), kind=kCustom, calls=%fused_computation.4 | custom fusion | flops 65536 | bytes 33280 | tf_op jit(solution)/shard_map/scatter-add | solution.py:60
  141.9 0.8 copy.16
  (4 shorter events, 0.1 us)
Async XLA Ops:
  6.5 39.9 %reduce-scatter.4.cloned.1.call-start = ((), (), s32[]{:S(2)}) async-start(), calls=%async_computation.1 | async-start | bytes 163840
Sparse Core Ops, SparseCore 0:
  11.8 22.3 reduce-scatter.3
where the time goes:
time: 150 us
  blocking collectives  73.3 us (49%)
  other arithmetic  56.2 us (37%)
  between operations  14.1 us (9%)
  local copies, waits for them, and re-layouts  3.09 us (2%)
  matrix products  2.81 us (2%)
    scatter-add x1, other arithmetic, per_device(): year_loss = empty.at[:, placed.reshape(-1)].add(repeated.T)  50.4 us
    all_gather x1, blocking collectives, per_device(): every_year = lax.all_gather(occurrence, 'ev', axis=0, tiled=True)  32.6 us
    all_gather x1, blocking collectives, per_device(): every_summary = lax.all_gather(own_summary, 'ev', axis=0, tiled=True)  30.6 us
    unnamed x1, blocking collectives  10.1 us
  transfers between devices with their start and end apart: 1, of which 0 were waited for; matrix products, arithmetic and copies ran while one was open for 1% of the time, Pallas kernels for 0%

commit v1 on v0

v1 whole, which is shorter than its diff:
```python
import functools

import jax
import jax.numpy as jnp
from jax import lax
from jax.experimental import pallas as pl
from jax.experimental.pallas import tpu as pltpu
from jax.sharding import PartitionSpec as P

SUMM = 32
YR_DEV = 1024
LANES = 128
FIELDS = 4
NT = (((1,), (1,)), ((), ()))


def lane_group(shape, width):
    return lax.broadcasted_iota(jnp.int32, shape, len(shape) - 1) // width


def sum_groups(x, width):
    step = width
    while step < LANES:
        x = x + pltpu.roll(x, step, x.ndim - 1)
        step *= 2
    return x


def pack_column(row, width, groups):
    n = row.shape[1]
    lo = n // groups
    eye = lax.broadcasted_iota(jnp.int32, (n, n), 0) == lax.broadcasted_iota(jnp.int32, (n, n), 1)
    column = jnp.sum(jnp.where(eye, row, 0.0), axis=1, keepdims=True)
    group = lane_group((lo, LANES), width)
    tile = jnp.zeros((lo, LANES), jnp.float32)
    for hi in range(groups):
        tile = jnp.where(group == hi, column[hi * lo : (hi + 1) * lo], tile)
    return tile


def split2(x):
    hi = x.astype(jnp.bfloat16)
    lo = (x - hi.astype(jnp.float32)).astype(jnp.bfloat16)
    return hi, lo


def kernel(
    n_ev,
    n_pol,
    chunks,
    ground_hbm,
    ded_hbm,
    lim_hbm,
    bp_hbm,
    pd_hbm,
    pl_hbm,
    sh_hbm,
    ps_hbm,
    occ_hbm,
    out_ref,
    ground,
    ded,
    lim,
    bp,
    pd,
    plim,
    share,
    psum,
    occ,
    totals,
    parts,
    params,
    occ_all,
    rows_all,
    yq_ref,
    inc_ref,
    count,
    in_sem,
    g_sem,
    pol_send,
    pol_recv,
    ev_send,
    ev_recv,
):
    me_ev = lax.axis_index("ev")
    me_pol = lax.axis_index("pol")
    blocks, events, _ = ground.shape
    groups = LANES // events
    per_owner = pd.shape[1]
    q_lo = per_owner // groups
    held = SUMM // n_pol
    occs = occ.shape[1]
    o_lo = occs // groups
    per = blocks // chunks

    pol_peers = [lax.rem(me_pol + d, n_pol) for d in range(1, n_pol)]
    ev_peers = [lax.rem(me_ev + d, n_ev) for d in range(1, n_ev)]
    mesh_id = pl.DeviceIdType.MESH

    small = []
    for k, (src, dst) in enumerate(
        (
            (ded_hbm, ded),
            (lim_hbm, lim),
            (bp_hbm, bp),
            (occ_hbm, occ),
            (pd_hbm, pd),
            (pl_hbm, plim),
            (sh_hbm, share),
            (ps_hbm, psum),
        )
    ):
        copy = pltpu.make_async_copy(src, dst, in_sem.at[k])
        copy.start()
        small.append(copy)
    large = []
    for c in range(chunks):
        span = pl.ds(c * per, per)
        copy = pltpu.make_async_copy(ground_hbm.at[span], ground.at[span], g_sem.at[c])
        copy.start()
        large.append(copy)

    barrier = pltpu.get_barrier_semaphore()
    for peer in ev_peers:
        pl.semaphore_signal(barrier, inc=1, device_id={"ev": peer}, device_id_type=mesh_id)
    for peer in pol_peers:
        pl.semaphore_signal(barrier, inc=1, device_id={"pol": peer}, device_id_type=mesh_id)

    for copy in small:
        copy.wait()

    params[me_pol, 0] = pack_column(pd[...], events, groups)
    params[me_pol, 1] = pack_column(plim[...], events, groups)
    params[me_pol, 2] = pack_column(share[...], events, groups)
    params[me_pol, 3] = pack_column(psum[...].astype(jnp.float32), events, groups)
    turned = jnp.transpose(occ[...])
    occ_all[me_ev] = jnp.concatenate(
        [turned[h * o_lo : (h + 1) * o_lo] for h in range(groups)], axis=1
    )

    ones = jnp.ones((16, LANES), jnp.bfloat16)
    sub = lax.broadcasted_iota(jnp.int32, (groups, LANES), 0)
    on_diagonal = sub == lane_group((groups, LANES), events)
    for c in range(chunks):
        large[c].wait()
        span = pl.ds(c * per, per)
        lower = ded[span].astype(jnp.float32)[:, None, :]
        upper = lim[span].astype(jnp.float32)[:, None, :]
        net = jnp.minimum(jnp.maximum(ground[span].astype(jnp.float32) - lower, 0.0), upper)
        hi, lo = split2(net.reshape(per * events, LANES))
        sums = lax.dot_general(
            ones, hi, NT, preferred_element_type=jnp.float32
        ) + lax.dot_general(ones, lo, NT, preferred_element_type=jnp.float32)
        for k in range(per // groups):
            tile = sums[:groups, k * LANES : (k + 1) * LANES]
            totals[pl.ds(c * per + k * groups, groups), :] = jnp.where(on_diagonal, tile, 0.0)

    hi, lo = split2(sum_groups(totals[...], events))
    member = (
        lax.broadcasted_iota(jnp.int32, (per_owner * n_pol, blocks), 0) == bp[...]
    ).astype(jnp.float32).astype(jnp.bfloat16)
    partial = jnp.dot(member, hi, preferred_element_type=jnp.float32) + jnp.dot(
        member, lo, preferred_element_type=jnp.float32
    )
    group = lane_group((q_lo, LANES), events)
    for j in range(n_pol):
        tile = jnp.zeros((q_lo, LANES), jnp.float32)
        for h in range(groups):
            first = j * per_owner + h * q_lo
            tile = jnp.where(group == h, partial[first : first + q_lo], tile)
        parts[me_pol, j] = tile

    pl.semaphore_wait(barrier, (n_ev - 1) + (n_pol - 1))

    def to_pol(ref, kind):
        copies = []
        for d, peer in enumerate(pol_peers):
            copy = pltpu.make_async_remote_copy(
                src_ref=ref.at[me_pol],
                dst_ref=ref.at[me_pol],
                send_sem=pol_send.at[kind, d],
                recv_sem=pol_recv.at[kind, d],
                device_id={"pol": peer},
                device_id_type=mesh_id,
            )
            copy.start()
            copies.append(copy)
        return copies

    def to_ev(ref, kind):
        copies = []
        for d, peer in enumerate(ev_peers):
            copy = pltpu.make_async_remote_copy(
                src_ref=ref.at[me_ev],
                dst_ref=ref.at[me_ev],
                send_sem=ev_send.at[kind, d],
                recv_sem=ev_recv.at[kind, d],
                device_id={"ev": peer},
                device_id_type=mesh_id,
            )
            copy.start()
            copies.append(copy)
        return copies

    part_copies = to_pol(parts, 0)
    param_copies = to_pol(params, 1)
    occ_copies = to_ev(occ_all, 0)

    for copy in param_copies:
        copy.wait_recv()
    for copy in part_copies:
        copy.wait_recv()

    base = (me_pol * held).astype(jnp.float32)
    losses, summaries = [], []
    for j in range(n_pol):
        policy_ground = parts[0, j]
        for source in range(1, n_pol):
            policy_ground = policy_ground + parts[source, j]
        losses.append(
            params[j, 2]
            * jnp.minimum(jnp.maximum(policy_ground - params[j, 0], 0.0), params[j, 1])
        )
        summaries.append(params[j, 3] - base)
    sums = []
    for s in range(held):
        tile = jnp.zeros((q_lo, LANES), jnp.float32)
        for j in range(n_pol):
            tile = tile + jnp.where(summaries[j] == float(s), losses[j], 0.0)
        sums.append(jnp.sum(tile, axis=0, keepdims=True))
    if held < groups:
        sums.append(jnp.zeros((groups - held, LANES), jnp.float32))
    by_summary = sum_groups(jnp.concatenate(sums, axis=0), events)
    rows_all[me_ev] = jnp.sum(jnp.where(on_diagonal, by_summary, 0.0), axis=0, keepdims=True)
    row_copies = to_ev(rows_all, 1)

    for copy in occ_copies:
        copy.wait_recv()
    first_year = me_ev * YR_DEV
    quarter = YR_DEV // FIELDS
    half = quarter // 2
    group = lane_group((o_lo, LANES), events)
    for c in range(n_ev // groups):
        tiles = [occ_all[c * groups + i] for i in range(groups)]
        for d in range(groups):
            mixed = tiles[0]
            for i in range(groups):
                mixed = jnp.where(group == (i - d) % groups, tiles[i], mixed)
            if d:
                mixed = pltpu.roll(mixed, d * events, 1)
            year = mixed - first_year
            inc = jnp.zeros_like(year)
            for f in range(FIELDS):
                inside = (year >= f * quarter) & (year < (f + 1) * quarter)
                inc = jnp.where(inside, 1 << (8 * f), inc)
            yq_ref[pl.ds(d * o_lo, o_lo), :] = year & (quarter - 1)
            inc_ref[pl.ds(d * o_lo, o_lo), :] = inc
        for part in range(2):
            rows = lax.broadcasted_iota(jnp.int32, (half, LANES), 0) + part * half

            def add(step, acc):
                for k in range(8):
                    at = pl.ds(step * 8 + k, 1)
                    acc = acc + jnp.where(rows == yq_ref[at, :], inc_ref[at, :], 0)
                return acc

            acc = lax.fori_loop(0, occs // 8, add, jnp.zeros((half, LANES), jnp.int32))
            for f in range(FIELDS):
                number = ((acc >> (8 * f)) & 255).astype(jnp.float32)
                count[c, pl.ds(f * quarter + part * half, half), :] = number.astype(jnp.bfloat16)

    for copy in row_copies:
        copy.wait_recv()
    gathered = rows_all[...].reshape(n_ev, LANES)
    away = (lane_group((groups, LANES), events) - sub) & (groups - 1)
    total = None
    for c in range(n_ev // groups):
        rows = gathered[c * groups : (c + 1) * groups]
        event_loss = jnp.where(away == 0, rows, 0.0)
        for d in range(1, groups):
            moved = pltpu.roll(pltpu.roll(rows, d * events, 1), groups - d, 0)
            event_loss = jnp.where(away == d, moved, event_loss)
        hi = event_loss.astype(jnp.bfloat16).astype(jnp.float32)
        rest = event_loss - hi
        mid = rest.astype(jnp.bfloat16).astype(jnp.float32)
        left = jnp.concatenate([hi, mid, rest - mid, jnp.zeros_like(hi)], axis=0)
        product = lax.dot_general(
            left.astype(jnp.bfloat16), count[c], NT, preferred_element_type=jnp.float32
        )
        value = product[:groups] + (product[groups : 2 * groups] + product[2 * groups : 3 * groups])
        total = value if total is None else total + value
    out_ref[...] = total[:held]

    for copy in part_copies + param_copies + occ_copies + row_copies:
        copy.wait_send()


def per_device(
    n_ev,
    n_pol,
    ground_up,
    loc_deductible,
    loc_limit,
    block_policy,
    policy_deductible,
    policy_limit,
    policy_share,
    policy_summary,
    occurrence,
):
    blocks, events, _ = ground_up.shape
    per_owner = policy_share.shape[0]
    occs = occurrence.shape[1]
    groups = LANES // events
    chunks = 4
    anywhere = pl.BlockSpec(memory_space=pl.ANY)
    f32, i32, bf16 = jnp.float32, jnp.int32, jnp.bfloat16
    dma = pltpu.SemaphoreType.DMA
    return pl.pallas_call(
        functools.partial(kernel, n_ev, n_pol, chunks),
        out_shape=jax.ShapeDtypeStruct((SUMM // n_pol, YR_DEV), f32),
        in_specs=[anywhere] * 9,
        out_specs=pl.BlockSpec(memory_space=pltpu.VMEM),
        scratch_shapes=[
            pltpu.VMEM(ground_up.shape, bf16),
            pltpu.VMEM(loc_deductible.shape, bf16),
            pltpu.VMEM(loc_limit.shape, bf16),
            pltpu.VMEM((1, blocks), i32),
            pltpu.VMEM((1, per_owner), f32),
            pltpu.VMEM((1, per_owner), f32),
            pltpu.VMEM((1, per_owner), f32),
            pltpu.VMEM((1, per_owner), i32),
            pltpu.VMEM(occurrence.shape, i32),
            pltpu.VMEM((blocks, LANES), f32),
            pltpu.VMEM((n_pol, n_pol, per_owner // groups, LANES), f32),
            pltpu.VMEM((n_pol, 4, per_owner // groups, LANES), f32),
            pltpu.VMEM((n_ev, occs // groups, LANES), i32),
            pltpu.VMEM((n_ev, 1, LANES), f32),
            pltpu.VMEM((occs, LANES), i32),
            pltpu.VMEM((occs, LANES), i32),
            pltpu.VMEM((n_ev // groups, YR_DEV, LANES), bf16),
            dma((8,)),
            dma((chunks,)),
            dma((2, n_pol - 1)),
            dma((2, n_pol - 1)),
            dma((2, n_ev - 1)),
            dma((2, n_ev - 1)),
        ],
        compiler_params=pltpu.CompilerParams(collective_id=0, has_side_effects=True),
        name="losses",
    )(
        ground_up,
        loc_deductible,
        loc_limit,
        block_policy.reshape(1, -1),
        policy_deductible.reshape(1, -1),
        policy_limit.reshape(1, -1),
        policy_share.reshape(1, -1),
        policy_summary.reshape(1, -1),
        occurrence,
    )


def solution(mesh):
    placed = (
        P("pol", "ev", None),
        P("pol", None),
        P("pol", None),
        P("pol"),
        P("pol"),
        P("pol"),
        P("pol"),
        P("pol"),
        P("ev", None),
    )
    body = functools.partial(per_device, mesh.shape["ev"], mesh.shape["pol"])
    return jax.shard_map(
        body, mesh=mesh, in_specs=placed, out_specs=P("pol", "ev"), check_vma=False
    )
```

time: 150 us -> 17.3 us (0.12)
  blocking collectives: 73.3 us -> 0 us
  other arithmetic: 56.2 us -> 0 us
  Pallas kernels: 0 us -> 15.7 us
  between operations: 14.1 us -> 0.01 us
  matrix products: 2.81 us -> 0 us
  local copies, waits for them, and re-layouts: 3.09 us -> 1.38 us
    all_gather x2 -> x0, blocking collectives: 63.2 us -> none  [the longest x1 32.6 us: per_device(): every_year = lax.all_gather(occurrence, 'ev', axis=0, tiled=True)]
    scatter-add x1 -> x0, other arithmetic: 50.4 us -> none  [per_device(): year_loss = empty.at[:, placed.reshape(-1)].add(repeated.T)]
    pallas_call x0 -> x1, Pallas kernels: none -> 15.7 us  [per_device(): pl.pallas_call(functools.partial(kernel, n_ev, n_pol, chunks), out_shape=...]
    unnamed x1 -> x0, blocking collectives: 10.1 us -> none
    mul x1 -> x0, other arithmetic: 2.55 us -> none  [per_device(): repeated = jnp.repeat(every_summary, every_year.shape[1], axis=0) * weight]
    unnamed x1 -> x0, matrix products: 1.83 us -> none
    reduce_sum x1 -> x0, other arithmetic: 1.63 us -> none  [block_totals(): return jnp.sum(net_loss, axis=2)]
    convert_element_type x3 -> x0, other arithmetic: 1.63 us -> none  [the longest x1 0.81 us: block_totals(): upper = loc_limit.astype(jnp.float32)[:, None, :]]
  transfers between devices with their start and end apart: 1 -> 0, of which waited for: 0 -> 0; matrix products, arithmetic and copies ran while one was open for 1% -> 0% of each run, Pallas kernels for 0% -> 0%
where the time goes in v1:
time: 17.3 us; the launch traced here: 17.1 us
  Pallas kernels  15.7 us (91%)
  local copies, waits for them, and re-layouts  1.38 us (8%)
    pallas_call x1, Pallas kernels, per_device(): pl.pallas_call(functools.partial(kernel, n_ev, n_pol, chunks), out_shape=...  15.7 us
    unnamed x1, local copies, waits for them, and re-layouts  1.38 us

profile of v1, /device:TPU:0, one launch (start us, length us, event | category | flops | bytes accessed | tf_op | source)
XLA Modules:
  0.0 17.1 jit_solution(17644354013184869754)
XLA Ops:
  0.0 15.7 %losses.1 = f32[8,1024]{1,0:T(8,128)} custom-call(bf16[192,16,128]{2,1,0:T(8,128)(2,1)} %ground_hbm.1, bf16[192,128]{1,0:T(8,128)(2,1)} %ded_hbm.1, bf16[192,128]{1,0:T(8,128)(2,1)} %lim_hbm.1, s32[1,192]{1,0:T(1,128)} %bitcast.5, f32[1,64]{1,0:T(1,128)} %bitcast.6, f32[1,64]{1,0:T(1,128)} %bitcast.7, f32[1,64]{1,0:T(1,128)} %bitcast.8, s32[1,64]{1,0:T(1,128)} %bitcast.9, ...), custom_call_target="tpu_custom_call" | custom-call | tf_op jit(solution)/shard_map/losses/pallas_call | solution.py:319
  15.7 1.4 %copy.11 = f32[8,1024]{1,0:T(8,128)} copy(f32[8,1024]{1,0:T(8,128)} %losses.1) | data formatting | bytes 65536

commit v2 on v1

--- a/solution.py
+++ b/solution.py
@@ -62,11 +62,9 @@
     ded,
     lim,
     bp,
-    pd,
-    plim,
-    share,
     psum,
     occ,
+    member,
     totals,
     parts,
     params,
@@ -86,7 +84,7 @@
     me_pol = lax.axis_index("pol")
     blocks, events, _ = ground.shape
     groups = LANES // events
-    per_owner = pd.shape[1]
+    per_owner = psum.shape[1]
     q_lo = per_owner // groups
     held = SUMM // n_pol
     occs = occ.shape[1]
@@ -104,9 +102,9 @@
             (lim_hbm, lim),
             (bp_hbm, bp),
             (occ_hbm, occ),
-            (pd_hbm, pd),
-            (pl_hbm, plim),
-            (sh_hbm, share),
+            (pd_hbm, params.at[me_pol, 0]),
+            (pl_hbm, params.at[me_pol, 1]),
+            (sh_hbm, params.at[me_pol, 2]),
             (ps_hbm, psum),
         )
     ):
@@ -129,16 +127,16 @@
     for copy in small:
         copy.wait()
 
-    params[me_pol, 0] = pack_column(pd[...], events, groups)
-    params[me_pol, 1] = pack_column(plim[...], events, groups)
-    params[me_pol, 2] = pack_column(share[...], events, groups)
-    params[me_pol, 3] = pack_column(psum[...].astype(jnp.float32), events, groups)
+    params[me_pol, 3] = psum[...].astype(jnp.float32)
+    member[...] = (
+        lax.broadcasted_iota(jnp.int32, member.shape, 0) == bp[...]
+    ).astype(jnp.float32).astype(jnp.bfloat16)
     turned = jnp.transpose(occ[...])
     occ_all[me_ev] = jnp.concatenate(
         [turned[h * o_lo : (h + 1) * o_lo] for h in range(groups)], axis=1
     )
 
-    ones = jnp.ones((16, LANES), jnp.bfloat16)
+    ones = jnp.ones((16, 2 * LANES), jnp.bfloat16)
     sub = lax.broadcasted_iota(jnp.int32, (groups, LANES), 0)
     on_diagonal = sub == lane_group((groups, LANES), events)
     for c in range(chunks):
@@ -148,19 +146,15 @@
         upper = lim[span].astype(jnp.float32)[:, None, :]
         net = jnp.minimum(jnp.maximum(ground[span].astype(jnp.float32) - lower, 0.0), upper)
         hi, lo = split2(net.reshape(per * events, LANES))
-        sums = lax.dot_general(
-            ones, hi, NT, preferred_element_type=jnp.float32
-        ) + lax.dot_general(ones, lo, NT, preferred_element_type=jnp.float32)
+        both = jnp.concatenate([hi, lo], axis=1)
+        sums = lax.dot_general(ones, both, NT, preferred_element_type=jnp.float32)
         for k in range(per // groups):
             tile = sums[:groups, k * LANES : (k + 1) * LANES]
             totals[pl.ds(c * per + k * groups, groups), :] = jnp.where(on_diagonal, tile, 0.0)
 
     hi, lo = split2(sum_groups(totals[...], events))
-    member = (
-        lax.broadcasted_iota(jnp.int32, (per_owner * n_pol, blocks), 0) == bp[...]
-    ).astype(jnp.float32).astype(jnp.bfloat16)
-    partial = jnp.dot(member, hi, preferred_element_type=jnp.float32) + jnp.dot(
-        member, lo, preferred_element_type=jnp.float32
+    partial = jnp.dot(member[...], hi, preferred_element_type=jnp.float32) + jnp.dot(
+        member[...], lo, preferred_element_type=jnp.float32
     )
     group = lane_group((q_lo, LANES), events)
     for j in range(n_pol):
@@ -202,12 +196,13 @@
             copies.append(copy)
         return copies
 
+    param_copies = to_pol(params, 1)
     part_copies = to_pol(parts, 0)
-    param_copies = to_pol(params, 1)
     occ_copies = to_ev(occ_all, 0)
 
     for copy in param_copies:
         copy.wait_recv()
+    packed = [[pack_column(params[j, k], events, groups) for k in range(4)] for j in range(n_pol)]
     for copy in part_copies:
         copy.wait_recv()
 
@@ -217,11 +212,9 @@
         policy_ground = parts[0, j]
         for source in range(1, n_pol):
             policy_ground = policy_ground + parts[source, j]
-        losses.append(
-            params[j, 2]
-            * jnp.minimum(jnp.maximum(policy_ground - params[j, 0], 0.0), params[j, 1])
-        )
-        summaries.append(params[j, 3] - base)
+        deductible, limit, share, summary = packed[j]
+        losses.append(share * jnp.minimum(jnp.maximum(policy_ground - deductible, 0.0), limit))
+        summaries.append(summary - base)
     sums = []
     for s in range(held):
         tile = jnp.zeros((q_lo, LANES), jnp.float32)
@@ -312,13 +305,13 @@
     per_owner = policy_share.shape[0]
     occs = occurrence.shape[1]
     groups = LANES // events
-    chunks = 4
+    chunks = 1
     anywhere = pl.BlockSpec(memory_space=pl.ANY)
     f32, i32, bf16 = jnp.float32, jnp.int32, jnp.bfloat16
     dma = pltpu.SemaphoreType.DMA
     return pl.pallas_call(
         functools.partial(kernel, n_ev, n_pol, chunks),
-        out_shape=jax.ShapeDtypeStruct((SUMM // n_pol, YR_DEV), f32),
+        out_shape=pltpu.VMEM((SUMM // n_pol, YR_DEV), f32),
         in_specs=[anywhere] * 9,
         out_specs=pl.BlockSpec(memory_space=pltpu.VMEM),
         scratch_shapes=[
@@ -326,14 +319,12 @@
             pltpu.VMEM(loc_deductible.shape, bf16),
             pltpu.VMEM(loc_limit.shape, bf16),
             pltpu.VMEM((1, blocks), i32),
-            pltpu.VMEM((1, per_owner), f32),
-            pltpu.VMEM((1, per_owner), f32),
-            pltpu.VMEM((1, per_owner), f32),
             pltpu.VMEM((1, per_owner), i32),
             pltpu.VMEM(occurrence.shape, i32),
+            pltpu.VMEM((per_owner * n_pol, blocks), bf16),
             pltpu.VMEM((blocks, LANES), f32),
             pltpu.VMEM((n_pol, n_pol, per_owner // groups, LANES), f32),
-            pltpu.VMEM((n_pol, 4, per_owner // groups, LANES), f32),
+            pltpu.VMEM((n_pol, 4, 1, per_owner), f32),
             pltpu.VMEM((n_ev, occs // groups, LANES), i32),
             pltpu.VMEM((n_ev, 1, LANES), f32),
             pltpu.VMEM((occs, LANES), i32),

time: 17.3 us -> 14.9 us (0.86)
  Pallas kernels: 15.7 us -> 14.2 us
  local copies, waits for them, and re-layouts: 1.38 us -> 0.62 us
    pallas_call x1, Pallas kernels: 15.7 us -> 14.2 us  [per_device(): pl.pallas_call(functools.partial(kernel, n_ev, n_pol, chunks), out_shape=...]
    unnamed x1, local copies, waits for them, and re-layouts: 1.38 us -> 0.62 us
where the time goes in v2:
time: 14.9 us; the launch traced here: 14.8 us
  Pallas kernels  14.2 us (95%)
  local copies, waits for them, and re-layouts  0.62 us (4%)
    pallas_call x1, Pallas kernels, per_device(): pl.pallas_call(functools.partial(kernel, n_ev, n_pol, chunks), out_shape=...  14.2 us
    unnamed x1, local copies, waits for them, and re-layouts  0.62 us

profile of v2, /device:TPU:0, one launch (start us, length us, event | category | flops | bytes accessed | tf_op | source)
XLA Modules:
  0.0 14.8 jit_solution(34358279479144685)
XLA Ops:
  0.0 14.2 %losses.1 = f32[8,1024]{1,0:T(8,128)S(1)} custom-call(bf16[192,16,128]{2,1,0:T(8,128)(2,1)} %ground_hbm.1, bf16[192,128]{1,0:T(8,128)(2,1)} %ded_hbm.1, bf16[192,128]{1,0:T(8,128)(2,1)} %lim_hbm.1, s32[1,192]{1,0:T(1,128)} %bitcast.5, f32[1,64]{1,0:T(1,128)} %bitcast.6, f32[1,64]{1,0:T(1,128)} %bitcast.7, f32[1,64]{1,0:T(1,128)} %bitcast.8, ...), custom_call_target="tpu_custom_call" | custom-call | tf_op jit(solution)/shard_map/losses/pallas_call | solution.py:312
  14.2 0.6 %copy.11 = f32[8,1024]{1,0:T(8,128)} copy(f32[8,1024]{1,0:T(8,128)S(1)} %losses.1) | data formatting | bytes 65536
